TPU v7x, 256 devices: a whole 4x4x8 slice. The times are simulated.
256 devices in a mesh: rep: 2 (over x_lo), tbl: 128 (over x_hi, y, z, core).
Axes of the slice: x: 4 (x_hi: 2, x_lo: 2; x = x_hi * 2 + x_lo), y: 4, z: 8, core: 2. Of those that a mesh axis runs over, the one named last changes fastest.
Arguments:
- embeddings: bfloat16 [1048576, 256], P('tbl'), may hold values from -6 to 6
- raw_ids: int32 [1024, 128, 60], P('tbl', 'rep'), may hold values from 0 to 16383
- id_weights: bfloat16 [1024, 128, 60], P('tbl', 'rep'), may hold values from 0.25 to 4
- lengths: int32 [1024, 128], P('tbl', 'rep'), may hold values from 1 to 60
- table_slot: int32 [128], replicated, may hold values from 0 to 127, each once
- table_rows: int32 [128], replicated, may hold values from 1 to 8192, 262144 in all
Outputs:
- pooled: float32 [1024, 128, 256], P('tbl', 'rep')
Inputs may be any that keep to these rules, and one draw needn't show every extreme that they name: The bag of request q for table k holds its first lengths[q, k] ids. `table_slot`: each slot holds exactly one table. `table_rows`: some table uses all 8192 rows of its slot.
All inputs are finite; a program needn't handle non-finite values.
Results may differ from a plain program's by a relative error of at most 0.0003.
Values sent between devices are 32-bit elements; how exact they have to be, the bound alone decides.
A program may use at most 64 MiB of HBM per device.

v0:
```python
import math

import jax
import jax.numpy as jnp
from jax import lax
from jax.sharding import PartitionSpec as P

TBL_DEV = 1
ROWS_SLOT = 8192


def in_one_piece(arrays, axis, split_dim, concat_dim, along):
    columns = [a.reshape(*a.shape[:along], -1) for a in arrays]
    both = jnp.concatenate(columns, axis=along)
    filled, at, done = (
        lax.all_to_all(both, axis, split_axis=split_dim, concat_axis=concat_dim, tiled=True),
        0,
        [],
    )
    for a, column in zip(arrays, columns):
        section = filled[..., at : at + column.shape[along]]
        done.append(section.reshape(*section.shape[:along], *a.shape[along:]))
        at += column.shape[along]
    return tuple(done)


def pool_block(embeddings, row_block, weight_block, len_block):
    picked = jnp.take(embeddings, row_block, axis=0)
    live = (
        lax.broadcasted_iota(jnp.int32, row_block.shape, row_block.ndim - 1) < len_block[..., None]
    )
    scaled = jnp.where(live, weight_block, jnp.zeros_like(weight_block))
    summed = jnp.einsum(
        "giqb,giqbd->giqd", scaled, picked.astype(jnp.float32), preferred_element_type=jnp.float32
    )
    divisor = jnp.maximum(len_block, 1).astype(jnp.float32)[..., None]
    return summed / divisor


def pool_rows(embeddings, targets, weighting, counts):
    sources, members, queries, positions = targets.shape
    blocking = math.gcd(sources, 16)
    shaped = targets.reshape(sources // blocking, blocking, members, queries, positions)
    weighted = weighting.reshape(sources // blocking, blocking, members, queries, positions)
    counted = counts.reshape(sources // blocking, blocking, members, queries)

    def pool_group(operands):
        return pool_block(embeddings, operands[0], operands[1], operands[2])

    pooled = lax.map(pool_group, (shaped, weighted, counted))
    return pooled.reshape(sources, members, queries, embeddings.shape[1])


def per_device(embeddings, raw_ids, id_weights, lengths, table_slot, table_rows):
    tables = table_slot.shape[0]
    shards = tables // TBL_DEV
    order = jnp.arange(tables, dtype=jnp.int32)
    slot_table = jnp.zeros((tables,), jnp.int32).at[table_slot].set(order)
    offsets = order % TBL_DEV * ROWS_SLOT
    sizes_by_slot = table_rows[slot_table]
    sent_ids = raw_ids.astype(jnp.float32)
    sent_weights = id_weights.astype(jnp.float32)
    sent_counts = lengths.astype(jnp.float32)
    hashed, weighting, counts = in_one_piece((sent_ids, sent_weights, sent_counts), "rep", 0, 1, 2)
    hashed = hashed.astype(jnp.int32)
    counts = counts.astype(jnp.int32)
    picked_ids = jnp.take(hashed, slot_table, axis=1)
    picked_weights = jnp.take(weighting, slot_table, axis=1)
    picked_counts = jnp.take(counts, slot_table, axis=1)
    queries = picked_ids.shape[0]
    width = picked_ids.shape[2]
    targets = offsets[None, :, None] + picked_ids % sizes_by_slot[None, :, None]
    targets = (
        jnp.transpose(targets, (1, 0, 2))
        .reshape(shards, TBL_DEV, queries, width)
        .astype(jnp.float32)
    )
    weights_sent = jnp.transpose(picked_weights, (1, 0, 2)).reshape(shards, TBL_DEV, queries, width)
    counts_sent = jnp.transpose(picked_counts).reshape(shards, TBL_DEV, queries).astype(jnp.float32)
    row_index = lax.all_to_all(targets, "tbl", split_axis=0, concat_axis=0, tiled=True).astype(
        jnp.int32
    )
    live_count = lax.all_to_all(counts_sent, "tbl", split_axis=0, concat_axis=0, tiled=True).astype(
        jnp.int32
    )
    pooled = pool_rows(
        embeddings,
        row_index,
        lax.all_to_all(weights_sent, "tbl", split_axis=0, concat_axis=0, tiled=True),
        live_count,
    )
    by_slot = lax.all_to_all(pooled, "tbl", split_axis=0, concat_axis=0, tiled=True)
    by_slot = by_slot.reshape(tables, queries, embeddings.shape[1])
    by_table = jnp.transpose(jnp.take(by_slot, table_slot, axis=0), (1, 0, 2))
    return lax.all_to_all(by_table, "rep", split_axis=1, concat_axis=0, tiled=True)


def solution(mesh):
    in_specs = (
        P("tbl", None),
        P("tbl", "rep", None),
        P("tbl", "rep", None),
        P("tbl", "rep"),
        P(),
        P(),
    )
    out_specs = P("tbl", "rep", None)
    return jax.shard_map(
        per_device, mesh=mesh, in_specs=in_specs, out_specs=out_specs, check_vma=False
    )
```

profile of v0, /device:TPU:1, one launch (start us, length us, event | category | flops | bytes accessed | tf_op | source)
XLA Modules:
  0.0 253.0 jit_solution(14122540634551298565)
XLA Ops:
  3.6 3.4 %all-to-all-start = ((f32[8,64,121]{2,1,0:T(8,128)}), f32[8,64,121]{2,1,0:T(8,128)S(1)}, u32[]{:S(2)}, u32[]{:S(2)}) async-start(f32[8,64,121]{2,1,0:T(8,128)} %copy.94), calls=%async_computation | async-start | bytes 524288 | tf_op jit(solution)/shard_map/all_to_all | solution.py:16
  9.4 2.3 all-to-all-done
  15.1 17.2 %all-to-all-start.1 = ((f32[128,1,4]{2,1,0:T(1,128)}), f32[128,1,4]{2,1,0:T(1,128)S(1)}, u32[]{:S(2)}, u32[]{:S(2)}) async-start(f32[128,1,4]{2,1,0:T(1,128)} %bitcast.14), calls=%async_computation.1 | async-start | bytes 131072 | tf_op jit(solution)/shard_map/all_to_all | solution.py:83
  32.3 5.7 %fusion.6 = f32[128,1,4,60]{3,2,1,0:T(4,128)S(1)} fusion(s32[128,4,60]{2,1,0:T(4,128)S(1)} %gather_fusion.3, s32[128]{0:T(128)S(1)} %compare_select_fusion.2, pred[128]{0:T(512)(128)(4,1)S(1)} %compare_and_fusion.1, pred[128]{0:T(512)(128)(4,1)S(1)} %broadcast_compare_fusion), kind=kLoop, calls=%fused_computation.26 | loop fusion | flops 276480 | bytes 246528 | tf_op jit(solution)/shard_map/convert_element_type | solution.py:76
  39.0 5.5 %all-to-all-done.1 = f32[128,1,4]{2,1,0:T(1,128)S(1)} async-done(((f32[128,1,4]{2,1,0:T(1,128)}), f32[128,1,4]{2,1,0:T(1,128)S(1)}, u32[]{:S(2)}, u32[]{:S(2)}) %all-to-all-start.1) | async-done | bytes 2080 | tf_op jit(solution)/shard_map/all_to_all | solution.py:83
  44.5 8.4 %all-to-all-start.3 = ((f32[128,1,240]{2,1,0:T(1,128)}), f32[128,1,240]{2,1,0:T(1,128)S(1)}, u32[]{:S(2)}, u32[]{:S(2)}) async-start(f32[128,1,240]{2,1,0:T(1,128)} %reshape.226), calls=%async_computation.3 | async-start | bytes 262144 | tf_op jit(solution)/shard_map/all_to_all | solution.py:80
  55.0 11.2 %all-to-all-done.3 = f32[128,1,240]{2,1,0:T(1,128)S(1)} async-done(((f32[128,1,240]{2,1,0:T(1,128)}), f32[128,1,240]{2,1,0:T(1,128)S(1)}, u32[]{:S(2)}, u32[]{:S(2)}) %all-to-all-start.3) | async-done | bytes 122912 | tf_op jit(solution)/shard_map/all_to_all | solution.py:80
  66.2 5.7 %all-to-all-start.2 = ((f32[128,1,240]{2,1,0:T(1,128)}), f32[128,1,240]{2,1,0:T(1,128)S(1)}, u32[]{:S(2)}, u32[]{:S(2)}) async-start(f32[128,1,240]{2,1,0:T(1,128)} %reshape.224), calls=%async_computation.2 | async-start | bytes 262144 | tf_op jit(solution)/shard_map/all_to_all | solution.py:89
  73.8 11.4 %all-to-all-done.2 = f32[128,1,240]{2,1,0:T(1,128)S(1)} async-done(((f32[128,1,240]{2,1,0:T(1,128)}), f32[128,1,240]{2,1,0:T(1,128)S(1)}, u32[]{:S(2)}, u32[]{:S(2)}) %all-to-all-start.2) | async-done | bytes 122912 | tf_op jit(solution)/shard_map/all_to_all | solution.py:89
  86.4 128.9 %while.10 = (s32[]{:T(128)}, f32[8,16,1,4,256]{4,3,2,1,0:T(4,128)}, s32[8,16,1,4]{1,3,2,0:T(4,128)S(1)}, f32[8,16,1,4,60]{4,3,2,1,0:T(4,128)S(1)}, s32[8,16,1,4,...) while((s32[]{:T(128)}, f32[8,16,1,4,256]{4,3,2,1,0:T(4,128)}, ...), condition=%wide.region_2.3_spmd, body=%wide.region_1.2_spmd.sunk | while | flops 3011970 | bytes 10207581 | solution.py:50
  86.7 11.1 %gather_fusion = bf16[3840,256]{1,0:T(8,128)(2,1)S(1)} fusion(bf16[8192,256]{1,0:T(8,128)(2,1)} %get-tuple-element.162, s32[4096]{0:T(1024)S(1)} %pad_clamp_fusion.4), kind=kCustom, calls=%fused_computation.clone.1 | custom fusion | bytes 3947520 | tf_op jit(solution)/shard_map/while/body/eval_jaxpr/jit(_take)/gather | solution.py:28
  97.8 1.5 gather.45
  99.4 2.3 fusion.15
  102.8 11.1 %gather_fusion = bf16[3840,256]{1,0:T(8,128)(2,1)S(1)} fusion(bf16[8192,256]{1,0:T(8,128)(2,1)} %get-tuple-element.162, s32[4096]{0:T(1024)S(1)} %pad_clamp_fusion.4), kind=kCustom, calls=%fused_computation.clone.1 | custom fusion | bytes 3947520 | tf_op jit(solution)/shard_map/while/body/eval_jaxpr/jit(_take)/gather | solution.py:28
  115.5 2.3 fusion.15
  118.9 11.1 %gather_fusion = bf16[3840,256]{1,0:T(8,128)(2,1)S(1)} fusion(bf16[8192,256]{1,0:T(8,128)(2,1)} %get-tuple-element.162, s32[4096]{0:T(1024)S(1)} %pad_clamp_fusion.4), kind=kCustom, calls=%fused_computation.clone.1 | custom fusion | bytes 3947520 | tf_op jit(solution)/shard_map/while/body/eval_jaxpr/jit(_take)/gather | solution.py:28
  130.0 1.5 gather.45
  131.6 2.3 fusion.15
  135.0 11.1 %gather_fusion = bf16[3840,256]{1,0:T(8,128)(2,1)S(1)} fusion(bf16[8192,256]{1,0:T(8,128)(2,1)} %get-tuple-element.162, s32[4096]{0:T(1024)S(1)} %pad_clamp_fusion.4), kind=kCustom, calls=%fused_computation.clone.1 | custom fusion | bytes 3947520 | tf_op jit(solution)/shard_map/while/body/eval_jaxpr/jit(_take)/gather | solution.py:28
  147.7 2.3 fusion.15
  151.2 11.1 %gather_fusion = bf16[3840,256]{1,0:T(8,128)(2,1)S(1)} fusion(bf16[8192,256]{1,0:T(8,128)(2,1)} %get-tuple-element.162, s32[4096]{0:T(1024)S(1)} %pad_clamp_fusion.4), kind=kCustom, calls=%fused_computation.clone.1 | custom fusion | bytes 3947520 | tf_op jit(solution)/shard_map/while/body/eval_jaxpr/jit(_take)/gather | solution.py:28
  163.8 2.3 fusion.15
  167.3 11.1 %gather_fusion = bf16[3840,256]{1,0:T(8,128)(2,1)S(1)} fusion(bf16[8192,256]{1,0:T(8,128)(2,1)} %get-tuple-element.162, s32[4096]{0:T(1024)S(1)} %pad_clamp_fusion.4), kind=kCustom, calls=%fused_computation.clone.1 | custom fusion | bytes 3947520 | tf_op jit(solution)/shard_map/while/body/eval_jaxpr/jit(_take)/gather | solution.py:28
  179.9 2.3 fusion.15
  183.4 11.1 %gather_fusion = bf16[3840,256]{1,0:T(8,128)(2,1)S(1)} fusion(bf16[8192,256]{1,0:T(8,128)(2,1)} %get-tuple-element.162, s32[4096]{0:T(1024)S(1)} %pad_clamp_fusion.4), kind=kCustom, calls=%fused_computation.clone.1 | custom fusion | bytes 3947520 | tf_op jit(solution)/shard_map/while/body/eval_jaxpr/jit(_take)/gather | solution.py:28
  196.0 2.3 fusion.15
  199.5 11.1 %gather_fusion = bf16[3840,256]{1,0:T(8,128)(2,1)S(1)} fusion(bf16[8192,256]{1,0:T(8,128)(2,1)} %get-tuple-element.162, s32[4096]{0:T(1024)S(1)} %pad_clamp_fusion.4), kind=kCustom, calls=%fused_computation.clone.1 | custom fusion | bytes 3947520 | tf_op jit(solution)/shard_map/while/body/eval_jaxpr/jit(_take)/gather | solution.py:28
  210.5 1.5 gather.45
  212.1 2.3 fusion.15
  215.2 5.6 %all-to-all-start.4 = ((f32[128,1,4,256]{3,2,1,0:T(4,128)}), f32[128,1,4,256]{3,2,1,0:T(4,128)S(1)}, u32[]{:S(2)}, u32[]{:S(2)}) async-start(f32[128,1,4,256]{3,2,1,0:T(4,128)} %bitcast.24), calls=%async_computation.4 | async-start | bytes 1048576 | tf_op jit(solution)/shard_map/all_to_all | solution.py:92
  220.8 20.0 %all-to-all-done.4 = f32[128,1,4,256]{3,2,1,0:T(4,128)S(1)} async-done(((f32[128,1,4,256]{3,2,1,0:T(4,128)}), f32[128,1,4,256]{3,2,1,0:T(4,128)S(1)}, u32[]{:S(2)}, u32[]{:S(2)}) %all-to-all-start.4) | async-done | bytes 524320 | tf_op jit(solution)/shard_map/all_to_all | solution.py:92
  242.0 10.1 %all_to_all.56 = f32[4,128,256]{2,0,1:T(4,128)S(1)} all-to-all(f32[4,128,256]{2,0,1:T(4,128)S(1)} %select_bitcast_fusion), channel_id=1, replica_groups=mesh['rep'=2,'tbl'=128] {'rep'}, dimensions={1} | all-to-all | bytes 1048576 | tf_op jit(solution)/shard_map/all_to_all | solution.py:95
  (124 shorter events, 34.1 us)
Async XLA Ops:
  0.0 8.1 %copy-start = (s32[128]{0:T(128)S(1)}, s32[128]{0:T(128)}, u32[]{:S(2)}) copy-start(s32[128]{0:T(128)} %param.13) | copy-start | bytes 1540
  0.0 7.0 %copy-start.1 = (s32[128]{0:T(128)S(1)}, s32[128]{0:T(128)}, u32[]{:S(2)}) copy-start(s32[128]{0:T(128)} %param.12) | copy-start | bytes 1540
  3.6 8.0 %all-to-all-start = ((f32[8,64,121]{2,1,0:T(8,128)}), f32[8,64,121]{2,1,0:T(8,128)S(1)}, u32[]{:S(2)}, u32[]{:S(2)}) async-start(f32[8,64,121]{2,1,0:T(8,128)} %copy.94), calls=%async_computation | async-start | bytes 524288 | tf_op jit(solution)/shard_map/all_to_all | solution.py:16
  15.1 29.4 %all-to-all-start.1 = ((f32[128,1,4]{2,1,0:T(1,128)}), f32[128,1,4]{2,1,0:T(1,128)S(1)}, u32[]{:S(2)}, u32[]{:S(2)}) async-start(f32[128,1,4]{2,1,0:T(1,128)} %bitcast.14), calls=%async_computation.1 | async-start | bytes 131072 | tf_op jit(solution)/shard_map/all_to_all | solution.py:83
  44.5 21.7 %all-to-all-start.3 = ((f32[128,1,240]{2,1,0:T(1,128)}), f32[128,1,240]{2,1,0:T(1,128)S(1)}, u32[]{:S(2)}, u32[]{:S(2)}) async-start(f32[128,1,240]{2,1,0:T(1,128)} %reshape.226), calls=%async_computation.3 | async-start | bytes 262144 | tf_op jit(solution)/shard_map/all_to_all | solution.py:80
  66.2 19.1 %all-to-all-start.2 = ((f32[128,1,240]{2,1,0:T(1,128)}), f32[128,1,240]{2,1,0:T(1,128)S(1)}, u32[]{:S(2)}, u32[]{:S(2)}) async-start(f32[128,1,240]{2,1,0:T(1,128)} %reshape.224), calls=%async_computation.2 | async-start | bytes 262144 | tf_op jit(solution)/shard_map/all_to_all | solution.py:89
  215.2 25.6 %all-to-all-start.4 = ((f32[128,1,4,256]{3,2,1,0:T(4,128)}), f32[128,1,4,256]{3,2,1,0:T(4,128)S(1)}, u32[]{:S(2)}, u32[]{:S(2)}) async-start(f32[128,1,4,256]{3,2,1,0:T(4,128)} %bitcast.24), calls=%async_computation.4 | async-start | bytes 1048576 | tf_op jit(solution)/shard_map/all_to_all | solution.py:92
where the time goes:
time: 254 us; the launch traced here: 253 us
  local copies, waits for them, and re-layouts  115 us (45%)
  waiting for transfers between devices  50.4 us (20%)
  starting transfers between devices  40.4 us (16%)
  other arithmetic  18.5 us (7%)
  matrix products  18.5 us (7%)
  blocking collectives  10.1 us (4%)
    gather x16, local copies, waits for them, and re-layouts, pool_block(): picked = jnp.take(embeddings, row_block, axis=0)  101 us
    all_to_all x1, waiting for transfers between devices, per_device(): lax.all_to_all(pooled, 'tbl', split_axis=0, concat_axis=0, tiled=True)  20 us
    dot_general x8, matrix products, pool_block(): jnp.einsum('giqb,giqbd->giqd', scaled, picked.astype(jnp.float32), prefer...  18.5 us
    all_to_all x1, starting transfers between devices, per_device(): lax.all_to_all(counts_sent, 'tbl', split_axis=0, concat_axis=0, tiled=True)  17.2 us
    all_to_all x1, waiting for transfers between devices, per_device(): lax.all_to_all(weights_sent, 'tbl', split_axis=0, concat_axis=0, tiled=True)  11.4 us
    all_to_all x1, waiting for transfers between devices, per_device(): lax.all_to_all(targets, 'tbl', split_axis=0, concat_axis=0, tiled=True)  11.2 us
    all_to_all x1, blocking collectives, per_device(): lax.all_to_all(by_table, 'rep', split_axis=1, concat_axis=0, tiled=True)  10.1 us
    all_to_all x1, starting transfers between devices, per_device(): lax.all_to_all(targets, 'tbl', split_axis=0, concat_axis=0, tiled=True)  8.42 us
  transfers between devices with their start and end apart: 5, of which 5 were waited for; matrix products, arithmetic and copies ran while one was open for 5% of the time, Pallas kernels for 0%

commit v1 on v0

v1 whole, which is shorter than its diff:
```python
import functools

import jax
import jax.numpy as jnp
from jax import lax
from jax.experimental import pallas as pl
from jax.experimental.pallas import tpu as pltpu
from jax.sharding import PartitionSpec as P

MESH = pl.DeviceIdType.MESH
F32, BF16, I32 = jnp.float32, jnp.bfloat16, jnp.int32
SLOTS = 128
BAG = 60
ROWS = 8192
LO = 256
HI = ROWS // LO
CHUNKS = 2
PER = 4 // CHUNKS


def dot_nt(a, b):
    return lax.dot_general(a, b, (((1,), (1,)), ((), ())), preferred_element_type=F32)


def split2(x):
    top = x.astype(BF16)
    return top, (x - top.astype(F32)).astype(BF16)


def build_rows(y_ref, ids_ref, wf_ref, len_ref, half):
    for q in range(4):
        req = 4 * half + q
        count = len_ref[pl.ds(req, 1), :]
        for h in range(2):
            n = 32 if h == 0 else BAG - 32
            start = req + 256 * h
            ids = ids_ref[pl.ds(start, n, stride=8), :].astype(F32)
            w = wf_ref[pl.ds(start, n, stride=8), :]
            pos = lax.broadcasted_iota(I32, (n, 64), 0) + 32 * h
            w = jnp.where(pos < count, w, 0.0)
            y_ref[pl.ds((h * 4 + q) * 32, n), :] = jnp.concatenate([ids, w], axis=1)
            if n < 32:
                y_ref[pl.ds((h * 4 + q) * 32 + n, 32 - n), :] = jnp.zeros((32 - n, 128), F32)


def to_slots(slot_of_lane, y_ref):
    row = lax.broadcasted_iota(I32, (256, 128), 0)
    lane = lax.broadcasted_iota(I32, (256, 128), 1)
    slot = jnp.where(row < 128, row, row - 128)
    pick = (slot_of_lane == slot) & ((row < 128) == (lane < 64))
    pick = jnp.where(pick, 1.0, 0.0).astype(BF16)
    top, rest = split2(y_ref[...])
    return dot_nt(pick, top) + dot_nt(pick, rest)


def place(out_ref, held, ch, half):
    for q in range(PER):
        for c in range(2):
            out_ref[4 * half + ch * PER + q, :, pl.ds(128 * c, 128)] = held[ch, :, 2 * q + c, :]


def kernel(
    ts_smem, ts_ref, tr_ref, ids_ref, w_ref, len_ref, emb_ref,
    out_ref,
    wf, y_own, y_send, y_recv, send1, recv1, key, low, wgt, count, table, acc,
    send2, p_send, p_recv, kept,
    emb_sem, rep_s, rep_r, a_s, a_r, b_s, b_r, c_s, c_r,
    *recv2,
):
    me = lax.axis_index("tbl")
    rep = lax.axis_index("rep")
    other = 1 - rep

    barrier = pltpu.get_barrier_semaphore()

    def greet(d, carry):
        peer = lax.rem(me + d, SLOTS)
        pl.semaphore_signal(barrier, inc=1, device_id={"tbl": peer}, device_id_type=MESH)
        return carry

    lax.fori_loop(1, SLOTS, greet, 0)
    pl.semaphore_signal(barrier, inc=1, device_id={"rep": other}, device_id_type=MESH)

    load = pltpu.make_async_copy(emb_ref, table, emb_sem)
    load.start()

    wf[...] = w_ref[...].astype(F32)
    build_rows(y_send, ids_ref, wf, len_ref, other)
    pl.semaphore_wait(barrier, SLOTS)
    swap = pltpu.make_async_remote_copy(
        y_send, y_recv, rep_s, rep_r, device_id={"rep": other}, device_id_type=MESH
    )
    swap.start()
    build_rows(y_own, ids_ref, wf, len_ref, rep)

    lane = lax.broadcasted_iota(I32, (1, 128), 1)
    slots = ts_ref[...]
    rolled = pltpu.roll(slots, 64, 1)
    first = jnp.where(lane < 64, slots, rolled)
    second = jnp.where(lane < 64, rolled, slots)
    mine = jnp.where(rep == 0, first, second)
    theirs = jnp.where(rep == 0, second, first)
    moved = to_slots(mine, y_own)
    swap.wait()
    moved = moved + to_slots(theirs, y_recv)
    for h in range(2):
        for part in range(2):
            send1[:, 2 * part + h, :] = moved[128 * part : 128 * part + 128, 128 * h : 128 * h + 128]

    def out1(d, carry):
        peer = lax.rem(me + d, SLOTS)
        pltpu.make_async_remote_copy(
            send1.at[peer], recv1.at[me], a_s, a_r, device_id={"tbl": peer}, device_id_type=MESH
        ).start()
        return carry

    lax.fori_loop(1, SLOTS, out1, 0)
    recv1[me] = send1[me]
    all1 = pltpu.make_async_remote_copy(
        send1.at[pl.ds(0, SLOTS - 1)], recv1.at[pl.ds(0, SLOTS - 1)], a_s, a_r,
        device_id={"rep": other}, device_id_type=MESH,
    )
    all1.wait_recv()
    all1.wait_send()

    rows = jnp.sum(jnp.where(slots == me, tr_ref[...], 0), axis=1, keepdims=True).astype(F32)
    src = lax.broadcasted_iota(I32, (128, 128), 0)
    col = lax.broadcasted_iota(I32, (128, 128), 1)
    bag = (4 * lax.rem(src, 2) + col // 32).astype(F32)
    for h in range(2):
        ids = recv1[:, h, :]
        times = jnp.floor((ids + 0.5) / rows)
        row = ids - times * rows
        row = jnp.where(row < 0.0, row + rows, row)
        row = jnp.where(row >= rows, row - rows, row)
        top = jnp.floor(row * (1.0 / LO))
        key[h] = top * 8.0 + bag
        low[h] = row - top * LO
        wgt[h] = recv1[:, 2 + h, :]

    line = lax.broadcasted_iota(I32, (256, 128), 0).astype(F32).astype(BF16)

    def spread(ref, h, t):
        x = jnp.broadcast_to(ref[h, pl.ds(t, 1), :], (16, 128)).astype(BF16)
        return jnp.concatenate([x] * 16, axis=0)

    def count_group(g, carry):
        for p in range(4):
            t = pl.multiple_of(8 * g, 8) + 2 * p
            total = None
            for h in range(2):
                left, right = [], []
                for i in range(2):
                    left.append(jnp.where(spread(key, h, t + i) == line, spread(wgt, h, t + i), jnp.bfloat16(0)))
                    right.append(jnp.where(spread(low, h, t + i) == line, jnp.bfloat16(1), jnp.bfloat16(0)))
                part = dot_nt(jnp.concatenate(left, axis=1), jnp.concatenate(right, axis=1))
                total = part if total is None else total + part
            at = pl.multiple_of(32 * g, 8) + 8 * p
            for c in range(2):
                count[c, :, pl.ds(at, 8), :] = total[:, 128 * c : 128 * c + 128].reshape(HI, 8, 128)
        return carry

    lax.fori_loop(0, SLOTS // 8, count_group, 0)
    load.wait()

    for ch in range(CHUNKS):
        for q in range(PER):
            req = ch * PER + q

            def pool(g, carry):
                total = None
                for i in range(8):
                    hi = 8 * g + i
                    x = jnp.concatenate([count[c, hi, pl.ds(req, 128, stride=4), :] for c in range(2)], axis=1)
                    top, rest = split2(x)
                    part = jnp.dot(
                        jnp.concatenate([top, rest], axis=0),
                        table[pl.ds(pl.multiple_of(hi * LO, LO), LO), :],
                        preferred_element_type=F32,
                    )
                    total = part if total is None else total + part

                @pl.when(g == 0)
                def _():
                    acc[...] = total

                @pl.when(g > 0)
                def _():
                    acc[...] += total

                return carry

            lax.fori_loop(0, HI // 8, pool, 0)
            for c in range(2):
                cols = pl.ds(128 * c, 128)
                send2[ch, :, 2 * q + c, :] = acc[pl.ds(0, 128), cols] + acc[pl.ds(128, 128), cols]

        def out2(d, carry):
            peer = lax.rem(me + d, SLOTS)
            pltpu.make_async_remote_copy(
                send2.at[ch, peer], recv2[ch].at[me], b_s.at[ch], b_r.at[ch],
                device_id={"tbl": peer}, device_id_type=MESH,
            ).start()
            return carry

        lax.fori_loop(1, SLOTS, out2, 0)
        recv2[ch][me] = send2[ch, me]

    swaps = []
    for ch in range(CHUNKS):
        all2 = pltpu.make_async_remote_copy(
            send2.at[ch, pl.ds(0, SLOTS - 1)], recv2[ch].at[pl.ds(0, SLOTS - 1)], b_s.at[ch], b_r.at[ch],
            device_id={"rep": other}, device_id_type=MESH,
        )
        all2.wait_recv()

        def give(k, carry):
            p_send[ch, k] = recv2[ch][ts_smem[64 * other + k]]
            return carry

        lax.fori_loop(0, 64, give, 0)
        swap = pltpu.make_async_remote_copy(
            p_send.at[ch], p_recv.at[ch], c_s.at[ch], c_r.at[ch], device_id={"rep": other}, device_id_type=MESH
        )
        swap.start()
        swaps.append(swap)

        def keep(k, carry):
            kept[ch, k] = recv2[ch][ts_smem[64 * rep + k]]
            return carry

        lax.fori_loop(0, 64, keep, 0)
        place(out_ref, kept, ch, rep)
        all2.wait_send()
    for ch in range(CHUNKS):
        swaps[ch].wait()
        place(out_ref, p_recv, ch, other)


def per_device(embeddings, raw_ids, id_weights, lengths, table_slot, table_rows):
    ids = jnp.transpose(raw_ids, (2, 0, 1)).reshape(8 * BAG, 64)
    weights = jnp.transpose(id_weights, (2, 0, 1)).reshape(8 * BAG, 64)
    vmem = pl.BlockSpec(memory_space=pltpu.VMEM)
    dma = pltpu.SemaphoreType.DMA
    sums = pl.pallas_call(
        kernel,
        out_shape=jax.ShapeDtypeStruct((8, 64, 256), F32),
        in_specs=[pl.BlockSpec(memory_space=pltpu.SMEM), vmem, vmem, vmem, vmem, vmem, pl.BlockSpec(memory_space=pl.ANY)],
        out_specs=vmem,
        scratch_shapes=[
            pltpu.VMEM((8 * BAG, 64), F32),
            pltpu.VMEM((256, 128), F32),
            pltpu.VMEM((256, 128), F32),
            pltpu.VMEM((256, 128), F32),
            pltpu.VMEM((SLOTS, 4, 128), F32),
            pltpu.VMEM((SLOTS, 4, 128), F32),
            pltpu.VMEM((2, 128, 128), F32),
            pltpu.VMEM((2, 128, 128), F32),
            pltpu.VMEM((2, 128, 128), F32),
            pltpu.VMEM((2, HI, 512, 128), F32),
            pltpu.VMEM((ROWS, 256), BF16),
            pltpu.VMEM((256, 256), F32),
            pltpu.VMEM((CHUNKS, SLOTS, 2 * PER, 128), F32),
            pltpu.VMEM((CHUNKS, 64, 2 * PER, 128), F32),
            pltpu.VMEM((CHUNKS, 64, 2 * PER, 128), F32),
            pltpu.VMEM((CHUNKS, 64, 2 * PER, 128), F32),
            dma, dma, dma, dma, dma,
            dma((CHUNKS,)), dma((CHUNKS,)), dma((CHUNKS,)), dma((CHUNKS,)),
        ]
        + [pltpu.VMEM((SLOTS, 2 * PER, 128), F32)] * CHUNKS,
        compiler_params=pltpu.CompilerParams(
            collective_id=0, has_side_effects=True, vmem_limit_bytes=61 * 1024 * 1024
        ),
    )(table_slot, table_slot.reshape(1, 128), table_rows.reshape(1, 128), ids, weights, lengths, embeddings)
    return sums / lengths.astype(F32)[..., None]


def solution(mesh):
    in_specs = (
        P("tbl", None),
        P("tbl", "rep", None),
        P("tbl", "rep", None),
        P("tbl", "rep"),
        P(),
        P(),
    )
    return jax.shard_map(
        per_device, mesh=mesh, in_specs=in_specs, out_specs=P("tbl", "rep", None), check_vma=False
    )
```

time: 254 us -> 66.6 us (0.26)
  local copies, waits for them, and re-layouts: 115 us -> 0 us
  Pallas kernels: 0 us -> 63.7 us
  waiting for transfers between devices: 50.4 us -> 0 us
  starting transfers between devices: 40.4 us -> 0 us
  matrix products: 18.5 us -> 0 us
  other arithmetic: 18.5 us -> 2.66 us
  blocking collectives: 10.1 us -> 0 us
    gather x21 -> x0, local copies, waits for them, and re-layouts: 105 us -> none  [the longest x16 101 us: pool_block(): picked = jnp.take(embeddings, row_block, axis=0)]
    pallas_call x0 -> x1, Pallas kernels: none -> 63.7 us  [per_device(): pl.pallas_call(kernel, out_shape=jax.ShapeDtypeStruct((8, 64, 256), F32),...]
    all_to_all x5 -> x0, waiting for transfers between devices: 50.4 us -> none  [the longest x1 20 us: per_device(): lax.all_to_all(pooled, 'tbl', split_axis=0, concat_axis=0, tiled=True)]
    all_to_all x5 -> x0, starting transfers between devices: 40.4 us -> none  [the longest x1 17.2 us: per_device(): lax.all_to_all(counts_sent, 'tbl', split_axis=0, concat_axis=0, tiled=True)]
    dot_general x8 -> x0, matrix products: 18.5 us -> none  [pool_block(): jnp.einsum('giqb,giqbd->giqd', scaled, picked.astype(jnp.float32), prefer...]
    all_to_all x1 -> x0, blocking collectives: 10.1 us -> none  [per_device(): lax.all_to_all(by_table, 'rep', split_axis=1, concat_axis=0, tiled=True)]
    convert_element_type x16 -> x1, other arithmetic: 8.55 us -> 0.69 us  [per_device(): return sums / lengths.astype(F32)[..., None]]
    dynamic_update_slice x8 -> x0, other arithmetic: 5.81 us -> none  [pool_rows(): pooled = lax.map(pool_group, (shaped, weighted, counted))]
  transfers between devices with their start and end apart: 5 -> 0, of which waited for: 5 -> 0; matrix products, arithmetic and copies ran while one was open for 5% -> 0% of each run, Pallas kernels for 0% -> 0%
where the time goes in v1:
time: 66.6 us; the launch traced here: 66.4 us
  Pallas kernels  63.7 us (96%)
  other arithmetic  2.66 us (4%)
    pallas_call x1, Pallas kernels, per_device(): pl.pallas_call(kernel, out_shape=jax.ShapeDtypeStruct((8, 64, 256), F32),...  63.7 us
    div x1, other arithmetic, per_device(): return sums / lengths.astype(F32)[..., None]  1.98 us

profile of v1, /device:TPU:1, one launch (start us, length us, event | category | flops | bytes accessed | tf_op | source)
XLA Modules:
  0.0 66.4 jit_solution(9747543190008721007)
XLA Ops:
  0.0 0.7 %convert_element_type.3 = f32[8,64]{1,0:T(8,128)S(1)} convert(s32[8,64]{1,0:T(8,128)} %len_ref.1) | non-fusion elementwise | flops 512 | bytes 4096 | tf_op jit(solution)/shard_map/convert_element_type | solution.py:275
  0.7 63.7 %shard_map.64 = f32[8,64,256]{2,1,0:T(8,128)} custom-call(s32[128]{0:T(128)} %ts_smem.1, s32[1,128]{1,0:T(1,128)} %bitcast.10, s32[1,128]{1,0:T(1,128)} %bitcast.11, s32[480,64]{1,0:T(8,128)} %bitcast.8, bf16[480,64]{1,0:T(8,128)(2,1)} %bitcast.9, s32[8,64]{1,0:T(8,128)} %len_ref.1, bf16[8192,256]{1,0:T(8,128)(2,1)} %emb_ref.1), custom_call_target="tpu_custom_call" | custom-call | tf_op jit(solution)/shard_map/pallas_call | solution.py:245
  64.4 2.0 %broadcast_divide_fusion = f32[8,64,256]{2,1,0:T(8,128)} fusion(f32[8,64,256]{2,1,0:T(8,128)} %shard_map.64, f32[8,64]{1,0:T(8,128)S(1)} %convert_element_type.3), kind=kLoop, calls=%fused_computation | loop fusion | flops 131072 | bytes 1050624 | tf_op jit(solution)/shard_map/div | solution.py:275

commit v2 on v1

v2 whole, which is shorter than its diff:
```python
import functools

import jax
import jax.numpy as jnp
from jax import lax
from jax.experimental import pallas as pl
from jax.experimental.pallas import tpu as pltpu
from jax.sharding import PartitionSpec as P

MESH = pl.DeviceIdType.MESH
F32, BF16, I32 = jnp.float32, jnp.bfloat16, jnp.int32
SLOTS = 128
BAG = 60
ROWS = 8192
LO = 256
HI = ROWS // LO
CHUNKS = ((0, 2), (2, 1), (3, 1))
MEMBERS = 16
GROUPS = SLOTS // MEMBERS
STEP = 8


def dot_nt(a, b):
    return lax.dot_general(a, b, (((1,), (1,)), ((), ())), preferred_element_type=F32)


def split2(x):
    top = x.astype(BF16)
    return top, (x - top.astype(F32)).astype(BF16)


def build_rows(y_ref, ids_ref, wf_ref, len_ref, half):
    for q in range(4):
        req = 4 * half + q
        count = len_ref[pl.ds(req, 1), :]
        for h in range(2):
            n = 32 if h == 0 else BAG - 32
            start = req + 256 * h
            ids = ids_ref[pl.ds(start, n, stride=8), :].astype(F32)
            w = wf_ref[pl.ds(start, n, stride=8), :]
            pos = lax.broadcasted_iota(I32, (n, 64), 0) + 32 * h
            w = jnp.where(pos < count, w, 0.0)
            y_ref[pl.ds((h * 4 + q) * 32, n), :] = jnp.concatenate([ids, w], axis=1)
            if n < 32:
                y_ref[pl.ds((h * 4 + q) * 32 + n, 32 - n), :] = jnp.zeros((32 - n, 128), F32)


def to_slots(slot_of_lane, y_ref):
    row = lax.broadcasted_iota(I32, (256, 128), 0)
    lane = lax.broadcasted_iota(I32, (256, 128), 1)
    slot = jnp.where(row < 128, row, row - 128)
    pick = (slot_of_lane == slot) & ((row < 128) == (lane < 64))
    pick = jnp.where(pick, 1.0, 0.0).astype(BF16)
    top, rest = split2(y_ref[...])
    return dot_nt(pick, top) + dot_nt(pick, rest)


def place(out_ref, held, inverse, half, first):
    for q in range(held.shape[1] // 2):
        req = 4 * half + first + q
        for c in range(2):
            out_ref[req, :, pl.ds(128 * c, 128)] = held[:, 2 * q + c, :] * inverse[req]


def identity(n):
    row = lax.broadcasted_iota(I32, (n, n), 0)
    return jnp.where(row == lax.broadcasted_iota(I32, (n, n), 1), 1.0, 0.0).astype(BF16)


def kernel(
    ts_smem, ts_ref, tr_ref, ids_ref, w_ref, len_ref, emb_ref,
    out_ref,
    wf, y_own, y_send, y_recv, send1, moved, recv1, key, turned, inverse, count, table, acc,
    emb_sem, rep_s, rep_r, a_s, a_r, b_s, b_r, c_s, c_r,
    *buffers,
):
    send2, recv2, p_send, p_recv, kept = (buffers[i :: 5] for i in range(5))
    me = lax.axis_index("tbl")
    rep = lax.axis_index("rep")
    other = 1 - rep
    group = me // MEMBERS

    barrier = pltpu.get_barrier_semaphore()

    def greet(d, carry):
        peer = lax.rem(me + d, SLOTS)
        pl.semaphore_signal(barrier, inc=1, device_id={"tbl": peer}, device_id_type=MESH)
        return carry

    lax.fori_loop(1, SLOTS, greet, 0)
    pl.semaphore_signal(barrier, inc=1, device_id={"rep": other}, device_id_type=MESH)

    load = pltpu.make_async_copy(emb_ref, table, emb_sem)
    load.start()

    wf[...] = w_ref[...].astype(F32)
    build_rows(y_send, ids_ref, wf, len_ref, other)
    build_rows(y_own, ids_ref, wf, len_ref, rep)
    lane = lax.broadcasted_iota(I32, (1, 128), 1)
    slots = ts_ref[...]
    rolled = pltpu.roll(slots, 64, 1)
    first = jnp.where(lane < 64, slots, rolled)
    second = jnp.where(lane < 64, rolled, slots)
    mine = jnp.where(rep == 0, first, second)
    theirs = jnp.where(rep == 0, second, first)
    moved[...] = to_slots(mine, y_own)
    columns = 1.0 / dot_nt(identity(64), len_ref[...].astype(F32).astype(BF16))
    for req in range(8):
        inverse[req] = jnp.broadcast_to(columns[:, req : req + 1], (64, 128))
    rows = jnp.sum(jnp.where(slots == me, tr_ref[...], 0), axis=1, keepdims=True).astype(F32)
    share = 1.0 / rows

    pl.semaphore_wait(barrier, SLOTS)
    swap = pltpu.make_async_remote_copy(
        y_send, y_recv, rep_s, rep_r, device_id={"rep": other}, device_id_type=MESH
    )
    swap.start()
    swap.wait()
    both = moved[...] + to_slots(theirs, y_recv)
    for h in range(2):
        for part in range(2):
            send1[:, 2 * part + h, :] = both[128 * part : 128 * part + 128, 128 * h : 128 * h + 128]

    def out1(d, carry):
        peer = lax.rem(me + d, SLOTS)
        pltpu.make_async_remote_copy(
            send1.at[peer], recv1.at[me], a_s, a_r.at[group], device_id={"tbl": peer}, device_id_type=MESH
        ).start()
        return carry

    lax.fori_loop(1, SLOTS, out1, 0)
    recv1[me] = send1[me]

    bag = (
        4 * lax.rem(lax.broadcasted_iota(I32, (MEMBERS, 4, 128), 0), 2)
        + lax.broadcasted_iota(I32, (MEMBERS, 4, 128), 2) // 32
    ).astype(F32)
    line = lax.broadcasted_iota(I32, (256, 128), 0).astype(F32).astype(BF16)
    along = lax.broadcasted_iota(I32, (128, 256), 1).astype(F32).astype(BF16)
    unit = identity(128)

    def arrived(n, where):
        return pltpu.make_async_remote_copy(
            send1.at[pl.ds(0, n)], recv1.at[pl.ds(0, n)], a_s, a_r.at[where],
            device_id={"rep": other}, device_id_type=MESH,
        )

    def spread(row):
        x = jnp.broadcast_to(row, (16, 128)).astype(BF16)
        return jnp.concatenate([x] * 16, axis=0)

    def count_group(src):
        base = src * MEMBERS
        ids = recv1[pl.ds(base, MEMBERS)]
        row = ids - jnp.floor((ids + 0.5) * share) * rows
        top = jnp.floor(row * (1.0 / LO))
        key[...] = top * 8.0 + bag
        low = (row - top * LO).reshape(4 * MEMBERS, 128)
        turned[...] = dot_nt(unit, low.astype(BF16))
        for p in range(MEMBERS // 2):
            left, right = [], []
            for h in range(2):
                for i in (2 * p, 2 * p + 1):
                    hit = spread(key[i, pl.ds(h, 1), :]) == line
                    left.append(jnp.where(hit, spread(recv1[base + i, pl.ds(2 + h, 1), :]), jnp.bfloat16(0)))
                    at = 4 * i + h
                    column = jnp.broadcast_to(turned[:, at : at + 1], (128, 256)).astype(BF16)
                    right.append(jnp.where(column == along, jnp.bfloat16(1), jnp.bfloat16(0)))
            total = jnp.dot(
                jnp.concatenate(left, axis=1), jnp.concatenate(right, axis=0), preferred_element_type=F32
            )
            at = pl.multiple_of(4 * MEMBERS * src, 8) + 8 * p
            for c in range(2):
                count[c, :, pl.ds(at, 8), :] = total[:, 128 * c : 128 * c + 128].reshape(HI, 8, 128)

    def count_step(d, carry):
        src = lax.rem(group + GROUPS - d, GROUPS)
        arrived(MEMBERS, src).wait_recv()
        count_group(src)
        return carry

    lax.fori_loop(1, GROUPS, count_step, 0)
    arrived(MEMBERS - 1, group).wait_recv()
    count_group(group)
    load.wait()

    for half in range(2):

        def pool(g, carry):
            total = None
            for i in range(STEP):
                hi = STEP * g + i
                stack = []
                for q in (2 * half, 2 * half + 1):
                    x = jnp.concatenate([count[c, hi, pl.ds(q, 128, stride=4), :] for c in range(2)], axis=1)
                    stack += split2(x)
                part = jnp.dot(
                    jnp.concatenate(stack, axis=0),
                    table[pl.ds(pl.multiple_of(hi * LO, LO), LO), :],
                    preferred_element_type=F32,
                )
                total = part if total is None else total + part

            @pl.when(g == 0)
            def _():
                acc[...] = total

            @pl.when(g > 0)
            def _():
                acc[...] += total

            return carry

        lax.fori_loop(0, HI // STEP, pool, 0)
        for ch, (at, size) in enumerate(CHUNKS):
            if at // 2 != half:
                continue
            for q in range(size):
                for c in range(2):
                    cols = pl.ds(128 * c, 128)
                    up = 256 * (at + q - 2 * half)
                    send2[ch][:, 2 * q + c, :] = acc[pl.ds(up, 128), cols] + acc[pl.ds(up + 128, 128), cols]

            def out2(d, carry):
                peer = lax.rem(me + d, SLOTS)
                pltpu.make_async_remote_copy(
                    send2[ch].at[peer], recv2[ch].at[me], b_s.at[ch], b_r.at[ch],
                    device_id={"tbl": peer}, device_id_type=MESH,
                ).start()
                return carry

            lax.fori_loop(1, SLOTS, out2, 0)
            recv2[ch][me] = send2[ch][me]

    arrived(SLOTS - 1, 0).wait_send()
    ends = []
    for ch, (at, size) in enumerate(CHUNKS):
        everyone = pltpu.make_async_remote_copy(
            send2[ch].at[pl.ds(0, SLOTS - 1)], recv2[ch].at[pl.ds(0, SLOTS - 1)], b_s.at[ch], b_r.at[ch],
            device_id={"rep": other}, device_id_type=MESH,
        )
        everyone.wait_recv()

        def give(k, carry):
            p_send[ch][k] = recv2[ch][ts_smem[64 * other + k]]
            return carry

        lax.fori_loop(0, 64, give, 0, unroll=8)
        back = pltpu.make_async_remote_copy(
            p_send[ch], p_recv[ch], c_s.at[ch], c_r.at[ch], device_id={"rep": other}, device_id_type=MESH
        )
        back.start()
        ends.append((everyone, back))

        def keep(k, carry):
            kept[ch][k] = recv2[ch][ts_smem[64 * rep + k]]
            return carry

        lax.fori_loop(0, 64, keep, 0, unroll=8)
        place(out_ref, kept[ch], inverse, rep, at)
    for ch, (at, size) in enumerate(CHUNKS):
        everyone, back = ends[ch]
        back.wait()
        place(out_ref, p_recv[ch], inverse, other, at)
        everyone.wait_send()


def per_device(embeddings, raw_ids, id_weights, lengths, table_slot, table_rows):
    ids = jnp.transpose(raw_ids, (2, 0, 1)).reshape(8 * BAG, 64)
    weights = jnp.transpose(id_weights, (2, 0, 1)).reshape(8 * BAG, 64)
    vmem = pl.BlockSpec(memory_space=pltpu.VMEM)
    dma = pltpu.SemaphoreType.DMA
    return pl.pallas_call(
        kernel,
        out_shape=jax.ShapeDtypeStruct((8, 64, 256), F32),
        in_specs=[pl.BlockSpec(memory_space=pltpu.SMEM), vmem, vmem, vmem, vmem, vmem, pl.BlockSpec(memory_space=pl.ANY)],
        out_specs=vmem,
        scratch_shapes=[
            pltpu.VMEM((8 * BAG, 64), F32),
            pltpu.VMEM((256, 128), F32),
            pltpu.VMEM((256, 128), F32),
            pltpu.VMEM((256, 128), F32),
            pltpu.VMEM((SLOTS, 4, 128), F32),
            pltpu.VMEM((256, 256), F32),
            pltpu.VMEM((SLOTS, 4, 128), F32),
            pltpu.VMEM((MEMBERS, 4, 128), F32),
            pltpu.VMEM((128, 4 * MEMBERS), F32),
            pltpu.VMEM((8, 64, 128), F32),
            pltpu.VMEM((2, HI, 512, 128), F32),
            pltpu.VMEM((ROWS, 256), BF16),
            pltpu.VMEM((512, 256), F32),
            dma, dma, dma, dma, dma((GROUPS,)),
            dma((len(CHUNKS),)), dma((len(CHUNKS),)), dma((len(CHUNKS),)), dma((len(CHUNKS),)),
        ]
        + [
            pltpu.VMEM((n, 2 * size, 128), F32)
            for _, size in CHUNKS
            for n in (SLOTS, SLOTS, 64, 64, 64)
        ],
        compiler_params=pltpu.CompilerParams(
            collective_id=0, has_side_effects=True, vmem_limit_bytes=61 * 1024 * 1024
        ),
    )(table_slot, table_slot.reshape(1, 128), table_rows.reshape(1, 128), ids, weights, lengths, embeddings)


def solution(mesh):
    in_specs = (
        P("tbl", None),
        P("tbl", "rep", None),
        P("tbl", "rep", None),
        P("tbl", "rep"),
        P(),
        P(),
    )
    return jax.shard_map(
        per_device, mesh=mesh, in_specs=in_specs, out_specs=P("tbl", "rep", None), check_vma=False
    )
```

time: 66.6 us -> 60.8 us (0.913)
  Pallas kernels: 63.7 us -> 58.7 us
  other arithmetic: 2.66 us -> 0 us
  local copies, waits for them, and re-layouts: 0 us -> 1.87 us
    pallas_call x1, Pallas kernels: 63.7 us -> 58.7 us  [per_device(): pl.pallas_call(kernel, out_shape=jax.ShapeDtypeStruct((8, 64, 256), F32),...]
    div x1 -> x0, other arithmetic: 1.98 us -> none  [per_device(): return sums / lengths.astype(F32)[..., None]]
    unnamed x0 -> x1, local copies, waits for them, and re-layouts: none -> 1.87 us
    convert_element_type x1 -> x0, other arithmetic: 0.69 us -> none  [per_device(): return sums / lengths.astype(F32)[..., None]]
where the time goes in v2:
time: 60.8 us; the launch traced here: 60.6 us
  Pallas kernels  58.7 us (97%)
  local copies, waits for them, and re-layouts  1.87 us (3%)
    pallas_call x1, Pallas kernels, per_device(): pl.pallas_call(kernel, out_shape=jax.ShapeDtypeStruct((8, 64, 256), F32),...  58.7 us
    unnamed x1, local copies, waits for them, and re-layouts  1.87 us

profile of v2, /device:TPU:1, one launch (start us, length us, event | category | flops | bytes accessed | tf_op | source)
XLA Modules:
  0.0 60.6 jit_solution(4367702840225157038)
XLA Ops:
  0.0 58.7 %shard_map.64 = f32[8,64,256]{2,1,0:T(8,128)} custom-call(s32[128]{0:T(128)} %ts_smem.1, s32[1,128]{1,0:T(1,128)} %bitcast.10, s32[1,128]{1,0:T(1,128)} %bitcast.11, s32[480,64]{1,0:T(8,128)} %bitcast.8, bf16[480,64]{1,0:T(8,128)(2,1)} %bitcast.9, s32[8,64]{1,0:T(8,128)} %len_ref.1, bf16[8192,256]{1,0:T(8,128)(2,1)} %emb_ref.1), custom_call_target="tpu_custom_call" | custom-call | tf_op jit(solution)/shard_map/pallas_call | solution.py:273
  58.7 1.9 %copy.8 = f32[8,64,256]{2,1,0:T(8,128)} copy(f32[8,64,256]{2,1,0:T(8,128)} %shard_map.64) | data formatting | bytes 1048576

commit v3 on v2

--- a/solution.py
+++ b/solution.py
@@ -17,7 +17,7 @@
 CHUNKS = ((0, 2), (2, 1), (3, 1))
 MEMBERS = 16
 GROUPS = SLOTS // MEMBERS
-STEP = 8
+STEP = 16
 
 
 def dot_nt(a, b):
@@ -62,6 +62,10 @@
             out_ref[req, :, pl.ds(128 * c, 128)] = held[:, 2 * q + c, :] * inverse[req]
 
 
+def by_z(slot):
+    return MEMBERS * (slot // 2 % GROUPS) + 2 * (slot // MEMBERS) + slot % 2
+
+
 def identity(n):
     row = lax.broadcasted_iota(I32, (n, n), 0)
     return jnp.where(row == lax.broadcasted_iota(I32, (n, n), 1), 1.0, 0.0).astype(BF16)
@@ -78,7 +82,9 @@
     me = lax.axis_index("tbl")
     rep = lax.axis_index("rep")
     other = 1 - rep
-    group = me // MEMBERS
+    mesh_z = lax.rem(me // 2, GROUPS)
+    in_z = 2 * (me // MEMBERS) + lax.rem(me, 2)
+    mine_at = MEMBERS * mesh_z + in_z
 
     barrier = pltpu.get_barrier_semaphore()
 
@@ -97,7 +103,7 @@
     build_rows(y_send, ids_ref, wf, len_ref, other)
     build_rows(y_own, ids_ref, wf, len_ref, rep)
     lane = lax.broadcasted_iota(I32, (1, 128), 1)
-    slots = ts_ref[...]
+    slots = by_z(ts_ref[...])
     rolled = pltpu.roll(slots, 64, 1)
     first = jnp.where(lane < 64, slots, rolled)
     second = jnp.where(lane < 64, rolled, slots)
@@ -107,7 +113,7 @@
     columns = 1.0 / dot_nt(identity(64), len_ref[...].astype(F32).astype(BF16))
     for req in range(8):
         inverse[req] = jnp.broadcast_to(columns[:, req : req + 1], (64, 128))
-    rows = jnp.sum(jnp.where(slots == me, tr_ref[...], 0), axis=1, keepdims=True).astype(F32)
+    rows = jnp.sum(jnp.where(slots == mine_at, tr_ref[...], 0), axis=1, keepdims=True).astype(F32)
     share = 1.0 / rows
 
     pl.semaphore_wait(barrier, SLOTS)
@@ -121,15 +127,34 @@
         for part in range(2):
             send1[:, 2 * part + h, :] = both[128 * part : 128 * part + 128, 128 * h : 128 * h + 128]
 
-    def out1(d, carry):
-        peer = lax.rem(me + d, SLOTS)
+    def near_first(send):
+        for far in range(GROUPS // 2 + 1):
+            ways = (far,) if far in (0, GROUPS // 2) else (far, GROUPS - far)
+
+            def one(d, carry):
+                at = lax.rem(in_z + d, MEMBERS)
+                for way in ways:
+                    there = lax.rem(mesh_z + way, GROUPS)
+                    send(MEMBERS * (at // 2) + 2 * there + lax.rem(at, 2), MEMBERS * there + at)
+                return carry
+
+            lax.fori_loop(1 if far == 0 else 0, MEMBERS, one, 0)
+
+    def in_turn(send):
+        def one(d, carry):
+            peer = lax.rem(me + d, SLOTS)
+            send(peer, MEMBERS * lax.rem(peer // 2, GROUPS) + 2 * (peer // MEMBERS) + lax.rem(peer, 2))
+            return carry
+
+        lax.fori_loop(1, SLOTS, one, 0)
+
+    def send_ids(peer, at):
         pltpu.make_async_remote_copy(
-            send1.at[peer], recv1.at[me], a_s, a_r.at[group], device_id={"tbl": peer}, device_id_type=MESH
+            send1.at[at], recv1.at[mine_at], a_s, a_r.at[mesh_z], device_id={"tbl": peer}, device_id_type=MESH
         ).start()
-        return carry
-
-    lax.fori_loop(1, SLOTS, out1, 0)
-    recv1[me] = send1[me]
+
+    near_first(send_ids)
+    recv1[mine_at] = send1[mine_at]
 
     bag = (
         4 * lax.rem(lax.broadcasted_iota(I32, (MEMBERS, 4, 128), 0), 2)
@@ -174,14 +199,15 @@
                 count[c, :, pl.ds(at, 8), :] = total[:, 128 * c : 128 * c + 128].reshape(HI, 8, 128)
 
     def count_step(d, carry):
-        src = lax.rem(group + GROUPS - d, GROUPS)
+        near = (d + 1) // 2
+        src = lax.rem(mesh_z + jnp.where(lax.rem(d, 2) == 1, near, GROUPS - near), GROUPS)
         arrived(MEMBERS, src).wait_recv()
         count_group(src)
         return carry
 
+    arrived(MEMBERS - 1, mesh_z).wait_recv()
+    count_group(mesh_z)
     lax.fori_loop(1, GROUPS, count_step, 0)
-    arrived(MEMBERS - 1, group).wait_recv()
-    count_group(group)
     load.wait()
 
     for half in range(2):
@@ -221,16 +247,14 @@
                     up = 256 * (at + q - 2 * half)
                     send2[ch][:, 2 * q + c, :] = acc[pl.ds(up, 128), cols] + acc[pl.ds(up + 128, 128), cols]
 
-            def out2(d, carry):
-                peer = lax.rem(me + d, SLOTS)
+            def send_sums(peer, at):
                 pltpu.make_async_remote_copy(
-                    send2[ch].at[peer], recv2[ch].at[me], b_s.at[ch], b_r.at[ch],
+                    send2[ch].at[at], recv2[ch].at[me], b_s.at[ch], b_r.at[ch],
                     device_id={"tbl": peer}, device_id_type=MESH,
                 ).start()
-                return carry
-
-            lax.fori_loop(1, SLOTS, out2, 0)
-            recv2[ch][me] = send2[ch][me]
+
+            in_turn(send_sums)
+            recv2[ch][me] = send2[ch][mine_at]
 
     arrived(SLOTS - 1, 0).wait_send()
     ends = []

time: 60.8 us -> 58.6 us (0.964)
  Pallas kernels: 58.7 us -> 56.6 us
    pallas_call x1, Pallas kernels: 58.7 us -> 56.6 us  [per_device(): pl.pallas_call(kernel, out_shape=jax.ShapeDtypeStruct((8, 64, 256), F32),...]
where the time goes in v3:
time: 58.6 us; the launch traced here: 58.4 us
  Pallas kernels  56.6 us (97%)
  local copies, waits for them, and re-layouts  1.87 us (3%)
    pallas_call x1, Pallas kernels, per_device(): pl.pallas_call(kernel, out_shape=jax.ShapeDtypeStruct((8, 64, 256), F32),...  56.6 us
    unnamed x1, local copies, waits for them, and re-layouts  1.87 us

profile of v3, /device:TPU:1, one launch (start us, length us, event | category | flops | bytes accessed | tf_op | source)
XLA Modules:
  0.0 58.4 jit_solution(12451254836770666072)
XLA Ops:
  0.0 56.6 %shard_map.64 = f32[8,64,256]{2,1,0:T(8,128)} custom-call(s32[128]{0:T(128)} %ts_smem.1, s32[1,128]{1,0:T(1,128)} %bitcast.10, s32[1,128]{1,0:T(1,128)} %bitcast.11, s32[480,64]{1,0:T(8,128)} %bitcast.8, bf16[480,64]{1,0:T(8,128)(2,1)} %bitcast.9, s32[8,64]{1,0:T(8,128)} %len_ref.1, bf16[8192,256]{1,0:T(8,128)(2,1)} %emb_ref.1), custom_call_target="tpu_custom_call" | custom-call | tf_op jit(solution)/shard_map/pallas_call | solution.py:297
  56.6 1.9 %copy.8 = f32[8,64,256]{2,1,0:T(8,128)} copy(f32[8,64,256]{2,1,0:T(8,128)} %shard_map.64) | data formatting | bytes 1048576

commit v4 on v3

--- a/solution.py
+++ b/solution.py
@@ -72,10 +72,10 @@
 
 
 def kernel(
-    ts_smem, ts_ref, tr_ref, ids_ref, w_ref, len_ref, emb_ref,
+    ts_smem, ts_hbm, tr_hbm, ids_hbm, w_hbm, len_hbm, emb_ref,
     out_ref,
     wf, y_own, y_send, y_recv, send1, moved, recv1, key, turned, inverse, count, table, acc,
-    emb_sem, rep_s, rep_r, a_s, a_r, b_s, b_r, c_s, c_r,
+    ts_ref, tr_ref, ids_ref, w_ref, len_ref, in_sem, emb_sem, rep_s, rep_r, a_s, a_r, b_s, b_r, c_s, c_r,
     *buffers,
 ):
     send2, recv2, p_send, p_recv, kept = (buffers[i :: 5] for i in range(5))
@@ -86,6 +86,14 @@
     in_z = 2 * (me // MEMBERS) + lax.rem(me, 2)
     mine_at = MEMBERS * mesh_z + in_z
 
+    inputs = [
+        pltpu.make_async_copy(src, dst, in_sem.at[i])
+        for i, (src, dst) in enumerate(
+            [(ids_hbm, ids_ref), (w_hbm, w_ref), (len_hbm, len_ref), (ts_hbm, ts_ref), (tr_hbm, tr_ref)]
+        )
+    ]
+    for copy in inputs:
+        copy.start()
     barrier = pltpu.get_barrier_semaphore()
 
     def greet(d, carry):
@@ -99,6 +107,8 @@
     load = pltpu.make_async_copy(emb_ref, table, emb_sem)
     load.start()
 
+    for copy in inputs:
+        copy.wait()
     wf[...] = w_ref[...].astype(F32)
     build_rows(y_send, ids_ref, wf, len_ref, other)
     build_rows(y_own, ids_ref, wf, len_ref, rep)
@@ -127,33 +137,30 @@
         for part in range(2):
             send1[:, 2 * part + h, :] = both[128 * part : 128 * part + 128, 128 * h : 128 * h + 128]
 
-    def near_first(send):
-        for far in range(GROUPS // 2 + 1):
-            ways = (far,) if far in (0, GROUPS // 2) else (far, GROUPS - far)
+    def to_all(send, phases):
+        for phase in phases:
+            slabs = [(way, lax.rem(mesh_z + way, GROUPS)) for way in phase]
+
+            def row(d, skip):
+                at = lax.rem(in_z + d, MEMBERS)
+                base = MEMBERS * (at // 2) + lax.rem(at, 2)
+                for way, there in slabs:
+                    if not (skip and way == 0):
+                        send(base + 2 * there, MEMBERS * there + at)
 
             def one(d, carry):
-                at = lax.rem(in_z + d, MEMBERS)
-                for way in ways:
-                    there = lax.rem(mesh_z + way, GROUPS)
-                    send(MEMBERS * (at // 2) + 2 * there + lax.rem(at, 2), MEMBERS * there + at)
+                row(d, False)
                 return carry
 
-            lax.fori_loop(1 if far == 0 else 0, MEMBERS, one, 0)
-
-    def in_turn(send):
-        def one(d, carry):
-            peer = lax.rem(me + d, SLOTS)
-            send(peer, MEMBERS * lax.rem(peer // 2, GROUPS) + 2 * (peer // MEMBERS) + lax.rem(peer, 2))
-            return carry
-
-        lax.fori_loop(1, SLOTS, one, 0)
+            row(0, True)
+            lax.fori_loop(1, MEMBERS, one, 0)
 
     def send_ids(peer, at):
         pltpu.make_async_remote_copy(
             send1.at[at], recv1.at[mine_at], a_s, a_r.at[mesh_z], device_id={"tbl": peer}, device_id_type=MESH
         ).start()
 
-    near_first(send_ids)
+    to_all(send_ids, ((1, 7, 0), (2, 6), (3, 5, 4)))
     recv1[mine_at] = send1[mine_at]
 
     bag = (
@@ -253,7 +260,7 @@
                     device_id={"tbl": peer}, device_id_type=MESH,
                 ).start()
 
-            in_turn(send_sums)
+            to_all(send_sums, ((4, 1, 7, 2, 6, 3, 5, 0),))
             recv2[ch][me] = send2[ch][mine_at]
 
     arrived(SLOTS - 1, 0).wait_send()
@@ -297,7 +304,7 @@
     return pl.pallas_call(
         kernel,
         out_shape=jax.ShapeDtypeStruct((8, 64, 256), F32),
-        in_specs=[pl.BlockSpec(memory_space=pltpu.SMEM), vmem, vmem, vmem, vmem, vmem, pl.BlockSpec(memory_space=pl.ANY)],
+        in_specs=[pl.BlockSpec(memory_space=pltpu.SMEM)] + [pl.BlockSpec(memory_space=pltpu.HBM)] * 6,
         out_specs=vmem,
         scratch_shapes=[
             pltpu.VMEM((8 * BAG, 64), F32),
@@ -313,6 +320,12 @@
             pltpu.VMEM((2, HI, 512, 128), F32),
             pltpu.VMEM((ROWS, 256), BF16),
             pltpu.VMEM((512, 256), F32),
+            pltpu.VMEM((1, 128), I32),
+            pltpu.VMEM((1, 128), I32),
+            pltpu.VMEM((8 * BAG, 64), I32),
+            pltpu.VMEM((8 * BAG, 64), BF16),
+            pltpu.VMEM((8, 64), I32),
+            dma((5,)),
             dma, dma, dma, dma, dma((GROUPS,)),
             dma((len(CHUNKS),)), dma((len(CHUNKS),)), dma((len(CHUNKS),)), dma((len(CHUNKS),)),
         ]

time: 58.6 us -> 57.2 us (0.976)
  Pallas kernels: 56.6 us -> 55.2 us
    pallas_call x1, Pallas kernels: 56.6 us -> 55.2 us  [per_device(): pl.pallas_call(kernel, out_shape=jax.ShapeDtypeStruct((8, 64, 256), F32),...]
where the time goes in v4:
time: 57.2 us; the launch traced here: 57.1 us
  Pallas kernels  55.2 us (97%)
  local copies, waits for them, and re-layouts  1.87 us (3%)
    pallas_call x1, Pallas kernels, per_device(): pl.pallas_call(kernel, out_shape=jax.ShapeDtypeStruct((8, 64, 256), F32),...  55.2 us
    unnamed x1, local copies, waits for them, and re-layouts  1.87 us

profile of v4, /device:TPU:1, one launch (start us, length us, event | category | flops | bytes accessed | tf_op | source)
XLA Modules:
  0.0 57.1 jit_solution(5314923402293458387)
XLA Ops:
  0.0 55.2 %shard_map.64 = f32[8,64,256]{2,1,0:T(8,128)} custom-call(s32[128]{0:T(128)} %ts_smem.1, s32[1,128]{1,0:T(1,128)} %bitcast.10, s32[1,128]{1,0:T(1,128)} %bitcast.11, s32[480,64]{1,0:T(8,128)} %bitcast.8, bf16[480,64]{1,0:T(8,128)(2,1)} %bitcast.9, s32[8,64]{1,0:T(8,128)} %len_hbm.1, bf16[8192,256]{1,0:T(8,128)(2,1)} %emb_ref.1), custom_call_target="tpu_custom_call" | custom-call | tf_op jit(solution)/shard_map/pallas_call | solution.py:304
  55.2 1.9 %copy.8 = f32[8,64,256]{2,1,0:T(8,128)} copy(f32[8,64,256]{2,1,0:T(8,128)} %shard_map.64) | data formatting | bytes 1048576

commit v5 on v4

--- a/solution.py
+++ b/solution.py
@@ -14,7 +14,8 @@
 ROWS = 8192
 LO = 256
 HI = ROWS // LO
-CHUNKS = ((0, 2), (2, 1), (3, 1))
+CHUNKS = ((0, 1), (1, 1), (2, 1), (3, 1))
+BLOCKS = ((0,), (1,), (2,), (3,))
 MEMBERS = 16
 GROUPS = SLOTS // MEMBERS
 STEP = 16
@@ -217,14 +218,15 @@
     lax.fori_loop(1, GROUPS, count_step, 0)
     load.wait()
 
-    for half in range(2):
+    for block in BLOCKS:
+        used = pl.ds(0, 256 * len(block))
 
         def pool(g, carry):
             total = None
             for i in range(STEP):
                 hi = STEP * g + i
                 stack = []
-                for q in (2 * half, 2 * half + 1):
+                for q in block:
                     x = jnp.concatenate([count[c, hi, pl.ds(q, 128, stride=4), :] for c in range(2)], axis=1)
                     stack += split2(x)
                 part = jnp.dot(
@@ -236,22 +238,22 @@
 
             @pl.when(g == 0)
             def _():
-                acc[...] = total
+                acc[used, :] = total
 
             @pl.when(g > 0)
             def _():
-                acc[...] += total
+                acc[used, :] += total
 
             return carry
 
         lax.fori_loop(0, HI // STEP, pool, 0)
         for ch, (at, size) in enumerate(CHUNKS):
-            if at // 2 != half:
+            if at not in block:
                 continue
             for q in range(size):
                 for c in range(2):
                     cols = pl.ds(128 * c, 128)
-                    up = 256 * (at + q - 2 * half)
+                    up = 256 * (at + q - block[0])
                     send2[ch][:, 2 * q + c, :] = acc[pl.ds(up, 128), cols] + acc[pl.ds(up + 128, 128), cols]
 
             def send_sums(peer, at):

time: 57.2 us -> 55.6 us (0.972)
  Pallas kernels: 55.2 us -> 53.6 us
    pallas_call x1, Pallas kernels: 55.2 us -> 53.6 us  [per_device(): pl.pallas_call(kernel, out_shape=jax.ShapeDtypeStruct((8, 64, 256), F32),...]
where the time goes in v5:
time: 55.6 us; the launch traced here: 55.5 us
  Pallas kernels  53.6 us (96%)
  local copies, waits for them, and re-layouts  1.87 us (3%)
    pallas_call x1, Pallas kernels, per_device(): pl.pallas_call(kernel, out_shape=jax.ShapeDtypeStruct((8, 64, 256), F32),...  53.6 us
    unnamed x1, local copies, waits for them, and re-layouts  1.87 us

profile of v5, /device:TPU:1, one launch (start us, length us, event | category | flops | bytes accessed | tf_op | source)
XLA Modules:
  0.0 55.5 jit_solution(505396468878749669)
XLA Ops:
  0.0 53.6 %shard_map.64 = f32[8,64,256]{2,1,0:T(8,128)} custom-call(s32[128]{0:T(128)} %ts_smem.1, s32[1,128]{1,0:T(1,128)} %bitcast.10, s32[1,128]{1,0:T(1,128)} %bitcast.11, s32[480,64]{1,0:T(8,128)} %bitcast.8, bf16[480,64]{1,0:T(8,128)(2,1)} %bitcast.9, s32[8,64]{1,0:T(8,128)} %len_hbm.1, bf16[8192,256]{1,0:T(8,128)(2,1)} %emb_ref.1), custom_call_target="tpu_custom_call" | custom-call | tf_op jit(solution)/shard_map/pallas_call | solution.py:306
  53.6 1.9 %copy.8 = f32[8,64,256]{2,1,0:T(8,128)} copy(f32[8,64,256]{2,1,0:T(8,128)} %shard_map.64) | data formatting | bytes 1048576

commit v6 on v5

--- a/solution.py
+++ b/solution.py
@@ -161,7 +161,7 @@
             send1.at[at], recv1.at[mine_at], a_s, a_r.at[mesh_z], device_id={"tbl": peer}, device_id_type=MESH
         ).start()
 
-    to_all(send_ids, ((1, 7, 0), (2, 6), (3, 5, 4)))
+    to_all(send_ids, ((0,), (1, 7), (2, 6), (3, 5), (4,)))
     recv1[mine_at] = send1[mine_at]
 
     bag = (

time: 55.6 us -> 56.2 us (1.011)
  Pallas kernels: 53.6 us -> 54.2 us
    pallas_call x1, Pallas kernels: 53.6 us -> 54.2 us  [per_device(): pl.pallas_call(kernel, out_shape=jax.ShapeDtypeStruct((8, 64, 256), F32),...]
where the time goes in v6:
time: 56.2 us; the launch traced here: 56.1 us
  Pallas kernels  54.2 us (96%)
  local copies, waits for them, and re-layouts  1.87 us (3%)
    pallas_call x1, Pallas kernels, per_device(): pl.pallas_call(kernel, out_shape=jax.ShapeDtypeStruct((8, 64, 256), F32),...  54.2 us
    unnamed x1, local copies, waits for them, and re-layouts  1.87 us

profile of v6, /device:TPU:1, one launch (start us, length us, event | category | flops | bytes accessed | tf_op | source)
XLA Modules:
  0.0 56.1 jit_solution(1993816333161422210)
XLA Ops:
  0.0 54.2 %shard_map.64 = f32[8,64,256]{2,1,0:T(8,128)} custom-call(s32[128]{0:T(128)} %ts_smem.1, s32[1,128]{1,0:T(1,128)} %bitcast.10, s32[1,128]{1,0:T(1,128)} %bitcast.11, s32[480,64]{1,0:T(8,128)} %bitcast.8, bf16[480,64]{1,0:T(8,128)(2,1)} %bitcast.9, s32[8,64]{1,0:T(8,128)} %len_hbm.1, bf16[8192,256]{1,0:T(8,128)(2,1)} %emb_ref.1), custom_call_target="tpu_custom_call" | custom-call | tf_op jit(solution)/shard_map/pallas_call | solution.py:306
  54.2 1.9 %copy.8 = f32[8,64,256]{2,1,0:T(8,128)} copy(f32[8,64,256]{2,1,0:T(8,128)} %shard_map.64) | data formatting | bytes 1048576
